TPU v7x, 32 devices: a whole 2x2x4 slice. The times are simulated.
32 devices in a mesh: sx: 4 (over x, core), sy: 4 (over z), dp: 2 (over y).
Axes of the slice: x: 2, y: 2, z: 4, core: 2. Of those that a mesh axis runs over, the one named last changes fastest.
Arguments:
- tokens: bfloat16 [2, 8192, 1280], P('dp', ('sx', 'sy')), may hold values from -6 to 6
- lengths: int32 [2, 64], P('dp'), may hold values from 1 to 512, 8192 in all within a row
- ln_gain: float32 [1280], replicated, may hold values from 0.1 to 1.9
- w_qkv: bfloat16 [1280, 3840], P('dp'), may hold values from -4 to 4, as said below
- w_out: bfloat16 [1280, 1280], P('dp'), may hold values from -0.15625 to 0.15625
Outputs:
- hidden: bfloat16 [2, 8192, 1280], P('dp', ('sx', 'sy'))
- pooled: float32 [2, 64, 1280], P('dp')
Inputs may be any that keep to these rules, and one draw needn't show every extreme that they name: The 64 lengths of a row sum to 8192; images are packed end to end in order. `w_qkv`: columns are queries, then keys, then values, each of 16 heads of 80 columns.
All inputs are finite; a program needn't handle non-finite values.
Results may differ from a plain program's by a relative error of at most 0.0051.
Values may be sent and summed in bfloat16 or wider, within the bound.
A program may use at most 128 MiB of HBM per device.

v0:
```python
import jax
import jax.numpy as jnp
from jax import lax
from jax.sharding import PartitionSpec as P

HEADS = 16
MAXLEN = 512


def with_halo(block, sides, width):
    for axis, dim in sides:
        count = lax.axis_size(axis)
        forward = [(i, i + 1) for i in range(count - 1)]
        backward = [(target, source) for source, target in forward]
        low = lax.ppermute(
            lax.slice_in_dim(block, block.shape[dim] - width, None, axis=dim), axis, forward
        )
        high = lax.ppermute(lax.slice_in_dim(block, 0, width, axis=dim), axis, backward)
        block = jnp.concatenate([low, block, high], axis=dim)
    return block


def image_ids(lengths, positions, total):
    offsets = jnp.cumsum(lengths) - lengths
    counted = jnp.sum((offsets[None, :] <= positions[:, None]).astype(jnp.int32), axis=1) - 1
    inside = (positions >= 0) & (positions < total)
    return jnp.where(inside, counted, -1)


def normalize(rows, ln_gain):
    values = rows.astype(jnp.float32)
    center = values - jnp.mean(values, axis=-1, keepdims=True)
    spread = jnp.mean(center * center, axis=-1, keepdims=True)
    return (center * lax.rsqrt(spread + 1e-05) * ln_gain).astype(jnp.bfloat16)


def attend(queries, keys, values, q_ids, k_ids):
    length = queries.shape[0]
    heads = queries.shape[1]
    block = min(512, length)
    scale = queries.shape[2] ** (-0.5)

    def one_block(index):
        allowed = q_ids[:, None] == k_ids[None, :]

        def one_head(head):
            q_head = lax.dynamic_index_in_dim(queries, head, 1, keepdims=False)
            k_head = lax.dynamic_index_in_dim(keys, head, 1, keepdims=False)
            v_head = lax.dynamic_index_in_dim(values, head, 1, keepdims=False)
            scores = jnp.dot(q_head, k_head.T, preferred_element_type=jnp.float32) * scale
            scores = jnp.where(allowed, scores, -1e30)
            top = jnp.max(scores, axis=1, keepdims=True)
            weights = jnp.exp(scores - top)
            probs = (weights / jnp.sum(weights, axis=1, keepdims=True)).astype(jnp.bfloat16)
            return jnp.dot(probs, v_head, preferred_element_type=jnp.float32).astype(jnp.bfloat16)

        outcome = lax.map(one_head, jnp.arange(heads, dtype=jnp.int32))
        return jnp.transpose(outcome, (1, 0, 2))

    blocks = lax.map(one_block, jnp.arange(length // block, dtype=jnp.int32))
    return blocks.reshape(length, heads, -1)


def shards(tokens, lengths, ln_gain, w_qkv, w_out):
    qkv_full, out_full = (
        lax.all_gather(w_qkv, "dp", axis=0, tiled=True),
        lax.all_gather(w_out, "dp", axis=0, tiled=True),
    )
    count_rows = tokens.shape[0]
    local = tokens.shape[1]
    width = tokens.shape[2]
    size = width // HEADS
    images = lengths.shape[1]
    count_x = lax.axis_size("sx")
    count_y = lax.axis_size("sy")
    total = local * count_x * count_y
    shard = lax.axis_index("sx") * count_y + lax.axis_index("sy")
    own_positions = shard * local + jnp.arange(local, dtype=jnp.int32)
    own_list = [image_ids(lengths[0], own_positions, total)]
    normed = normalize(tokens, ln_gain)
    qkv = jnp.dot(
        normed.reshape(count_rows * local, width), qkv_full, preferred_element_type=jnp.float32
    )
    qkv = qkv.astype(jnp.bfloat16).reshape(count_rows, local, 3 * width)
    pieces = qkv.reshape(count_rows, local, 3, HEADS, size)
    keyvals = with_halo(pieces[:, :, 1:3], ((("sx", "sy"), 1),), MAXLEN)
    k_pos = shard * local - MAXLEN + jnp.arange(local + 2 * MAXLEN, dtype=jnp.int32)
    rowidx = 0
    k_ids = image_ids(lengths[rowidx], k_pos, total)
    outcomes = [
        attend(
            pieces[rowidx, :, 0],
            keyvals[rowidx, :, 0],
            keyvals[rowidx, :, 1],
            own_list[rowidx],
            k_ids,
        )
    ]
    context = jnp.stack(outcomes, axis=0).reshape(count_rows * local, width)
    mixed = jnp.dot(context, out_full, preferred_element_type=jnp.float32).reshape(
        count_rows, local, width
    )
    hidden = (tokens.astype(jnp.float32) + mixed).astype(jnp.bfloat16)
    labels = jnp.arange(images, dtype=jnp.int32)
    rowidx = 0
    onehot = (labels[:, None] == own_list[rowidx][None, :]).astype(jnp.bfloat16)
    parts_list = [jnp.dot(onehot, hidden[rowidx], preferred_element_type=jnp.float32)]
    terms = jnp.stack(parts_list, axis=0)
    sums = lax.psum(terms, ("sx", "sy"))
    pooled = sums / lengths.astype(jnp.float32)[:, :, None]
    return (hidden, pooled)


def solution(mesh):
    in_specs = (P("dp", ("sx", "sy"), None), P("dp", None), P(), P("dp", None), P("dp", None))
    out_specs = (P("dp", ("sx", "sy"), None), P("dp", None, None))
    return jax.shard_map(shards, mesh=mesh, in_specs=in_specs, out_specs=out_specs, check_vma=False)
```

profile of v0, /device:TPU:8, one launch (start us, length us, event | category | flops | bytes accessed | tf_op | source)
XLA Modules:
  0.0 491.2 jit_solution(5797661446178218919)
XLA Ops:
  9.2 123.8 %all-gather.3.cloned.1.call-done = bf16[1280,3840]{1,0:T(8,128)(2,1)} async-done(((bf16[640,3840]{1,0:T(8,128)(2,1)}), bf16[1280,3840]{1,0:T(8,128)(2,1)}) %all-gather.3.cloned.1.call-update) | async-done | bytes 9830416 | tf_op jit(solution)/shard_map/all_gather | solution.py:66
  133.0 10.9 %convolution_convert_fusion = bf16[512,3840]{1,0:T(8,128)(2,1)} fusion(bf16[1280,3840]{1,0:T(8,128)(2,1)} %all-gather.3.cloned.1.call-done, bf16[1,512,1280]{2,1,0:T(8,128)(2,1)S(1)} %copy-done, f32[1280]{0:T(1024)S(1)} %copy-done.4, f32[512]{0:T(512)S(1)} %add_rsqrt_fusion, f32[512]{0:T(512)S(1)} %broadcast_multiply_fusion), kind=kOutput, calls=%fused_computation.19 | convolution fusion | flops 5038407680 | bytes 15082496 | tf_op jit(solution)/shard_map/dot_general | solution.py:81
  144.0 6.3 %copy.10 = bf16[512,3840]{0,1:T(8,128)(2,1)} copy(bf16[512,3840]{1,0:T(8,128)(2,1)} %convolution_convert_fusion) | data formatting | bytes 7864320 | tf_op jit(solution)/shard_map/convert_element_type | solution.py:84
  150.3 1.9 slice.17
  152.2 2.5 collective-permute-start.1
  154.7 3.4 collective-permute-start
  158.7 2.5 slice_bitcast_fusion.2
  161.2 51.9 %collective-permute-done.1 = bf16[1,512,2,16,80]{1,4,3,2,0:T(8,128)(2,1)} collective-permute-done((bf16[1,512,2,16,80]{1,4,3,2,0:T(8,128)(2,1)S(1)}, bf16[1,512,2,16,80]{1,4,3,2,0:T(8,128)(2,1)}, u32[]{:S(2)}, u32[]{:S(2)}) %collective-permute-start.1) | collective-permute-done | bytes 2621472 | tf_op jit(solution)/shard_map/ppermute | solution.py:18
  213.0 28.8 %collective-permute-done = bf16[1,512,2,16,80]{1,4,3,2,0:T(8,128)(2,1)} collective-permute-done((bf16[1,512,2,16,80]{1,4,3,2,0:T(8,128)(2,1)S(1)}, bf16[1,512,2,16,80]{1,4,3,2,0:T(8,128)(2,1)}, u32[]{:S(2)}, u32[]{:S(2)}) %collective-permute-start) | collective-permute-done | bytes 2621472 | tf_op jit(solution)/shard_map/ppermute | solution.py:15
  241.8 3.4 pad_maximum_fusion
  245.3 3.4 slice_bitcast_fusion
  248.6 106.8 %while.18 = (s32[]{:T(128)}, bf16[16,512,80]{1,2,0:T(8,128)(2,1)S(1)}, s32[16]{0:T(128)S(1)}, bf16[512,16,80]{0,2,1:T(8,128)(2,1)}, bf16[1536,16,80]{0,2,1:T(8,1...) while((s32[]{:T(128)}, ...), condition=%wide.region_8.9_spmd.clone, body=%wide.region_5.8_spmd.clone.sunk | while | flops 258776064 | bytes 10112171 | solution.py:57
  253.5 1.8 fusion.40
  260.2 1.8 fusion.40
  266.8 1.8 fusion.40
  273.5 1.8 fusion.40
  280.2 1.8 fusion.40
  286.9 1.8 fusion.40
  293.6 1.8 fusion.40
  300.2 1.8 fusion.40
  306.9 1.8 fusion.40
  313.6 1.8 fusion.40
  320.3 1.8 fusion.40
  326.9 1.8 fusion.40
  333.6 1.8 fusion.40
  340.3 1.8 fusion.40
  347.0 1.8 fusion.40
  351.3 1.8 fusion.38
  353.7 1.8 fusion.40
  356.5 4.2 fusion.18
  361.9 120.9 %all-reduce.2.cloned.1.call-done = f32[1,64,1280]{2,1,0:T(8,128)} async-done(((f32[1,64,1280]{2,1,0:T(8,128)}), f32[1,64,1280]{2,1,0:T(8,128)}) %all-reduce.2.cloned.1.call-update) | async-done | bytes 327696 | tf_op jit(solution)/shard_map/psum | solution.py:109
  482.9 1.8 broadcast_divide_fusion
  (83 shorter events, 49.7 us)
Async XLA Ops:
  7.2 1.3 copy-start
  7.2 125.9 %copy-start.4 = (f32[1280]{0:T(1024)S(1)}, f32[1280]{0:T(1024)}, u32[]{:S(2)}) copy-start(f32[1280]{0:T(1024)} %param.9) | copy-start | bytes 15364
  7.2 125.9 %all-gather.3.cloned.1.call-start = ((), (), s32[]{:S(2)}) async-start(), calls=%async_computation | async-start | bytes 14745600 | tf_op jit(solution)/shard_map/all_gather | solution.py:66
  7.9 347.6 %all-gather.5.cloned.1.call-start = ((), (), s32[]{:S(2)}) async-start(), calls=%async_computation.1 | async-start | bytes 4915200 | tf_op jit(solution)/shard_map/all_gather | solution.py:67
  150.3 7.9 %copy-start.3 = (s32[1,64]{1,0:T(1,128)S(1)}, s32[1,64]{1,0:T(1,128)}, u32[]{:S(2)}) copy-start(s32[1,64]{1,0:T(1,128)} %param.8) | copy-start | bytes 772
  152.2 60.8 %collective-permute-start.1 = (bf16[1,512,2,16,80]{1,4,3,2,0:T(8,128)(2,1)S(1)}, bf16[1,512,2,16,80]{1,4,3,2,0:T(8,128)(2,1)}, u32[]{:S(2)}, u32[]{:S(2)}) collective-permute-start(bf16[1,512,2,16,80]{1,4,3,2,0:T(8,128)(2,1)S(1)} %slice.17), channel_id=1, source_target_pairs={{2,0},{4,2},{6,4},{8,6},{10,8},{12,10},{14,12},{16,14},{18,16},{20... | collective-permute-start | bytes 7864328 | tf_op jit(solution)/shard_map/ppermute | solution.py:18
  154.7 87.1 %collective-permute-start = (bf16[1,512,2,16,80]{1,4,3,2,0:T(8,128)(2,1)S(1)}, bf16[1,512,2,16,80]{1,4,3,2,0:T(8,128)(2,1)}, u32[]{:S(2)}, u32[]{:S(2)}) collective-permute-start(bf16[1,512,2,16,80]{1,4,3,2,0:T(8,128)(2,1)S(1)} %slice.17), channel_id=1, source_target_pairs={{0,2},{2,4},{4,6},{6,8},{8,10},{10,12},{12,14},{14,16},{16,18},{18... | collective-permute-start | bytes 7864328 | tf_op jit(solution)/shard_map/ppermute | solution.py:15
  158.1 324.8 %all-reduce.2.cloned.1.call-start = ((), (), s32[]{:S(2)}) async-start(), calls=%async_computation.2 | async-start | bytes 655360 | tf_op jit(solution)/shard_map/psum | solution.py:109
  245.2 3.4 copy-start.5
  248.6 107.9 %copy-start.1 = (bf16[1,512,1280]{2,1,0:T(8,128)(2,1)S(1)}, bf16[1,512,1280]{2,1,0:T(8,128)(2,1)}, u32[]{:S(2)}) copy-start(bf16[1,512,1280]{2,1,0:T(8,128)(2,1)} %param.7) | copy-start | bytes 3932164
  355.5 1.1 copy-start.6
  360.8 123.9 %copy-start.2 = (bf16[1,512,1280]{2,1,0:T(8,128)(2,1)}, bf16[1,512,1280]{2,1,0:T(8,128)(2,1)S(1)}, u32[]{:S(2)}) copy-start(bf16[1,512,1280]{2,1,0:T(8,128)(2,1)S(1)} %fusion.18) | copy-start | bytes 3932164
Sparse Core Ops, SparseCore 0:
  9.6 123.4 all-gather.2
  158.2 47.8 all-gather.4
  362.1 120.7 all-reduce.1
where the time goes:
time: 493 us; the launch traced here: 491 us
  waiting for transfers between devices  326 us (66%)
  matrix products  73.3 us (15%)
  loops' own time  31.3 us (6%)
  local copies, waits for them, and re-layouts  25 us (5%)
  other arithmetic  15.6 us (3%)
  between operations  13.9 us (3%)
  starting transfers between devices  5.96 us (1%)
    all_gather x1, waiting for transfers between devices, shards(): lax.all_gather(w_qkv, 'dp', axis=0, tiled=True)  124 us
    psum x1, waiting for transfers between devices, shards(): sums = lax.psum(terms, ('sx', 'sy'))  121 us
    ppermute x1, waiting for transfers between devices, with_halo(): lax.ppermute(lax.slice_in_dim(block, 0, width, axis=dim), axis, backward)  51.9 us
    another operation x1, loops' own time, one_block(): outcome = lax.map(one_head, jnp.arange(heads, dtype=jnp.int32))  31.3 us
    dot_general x16, matrix products, one_head(): jnp.dot(probs, v_head, preferred_element_type=jnp.float32)  28.9 us
    ppermute x1, waiting for transfers between devices, with_halo(): lax.ppermute(lax.slice_in_dim(block, block.shape[dim] - width, None, axis...  28.8 us
    dot_general x16, matrix products, one_head(): jnp.dot(q_head, k_head.T, preferred_element_type=jnp.float32) * scale  28.1 us
    dot_general x1, matrix products, shards(): jnp.dot(normed.reshape(count_rows * local, width), qkv_full, preferred_el...  10.9 us
  transfers between devices with their start and end apart: 5, of which 4 were waited for; matrix products, arithmetic and copies ran while one was open for 18% of the time, Pallas kernels for 0%

commit v1 on v0

--- a/solution.py
+++ b/solution.py
@@ -106,7 +106,7 @@
     onehot = (labels[:, None] == own_list[rowidx][None, :]).astype(jnp.bfloat16)
     parts_list = [jnp.dot(onehot, hidden[rowidx], preferred_element_type=jnp.float32)]
     terms = jnp.stack(parts_list, axis=0)
-    sums = lax.psum(terms, ("sx", "sy"))
+    sums = lax.psum(lax.psum(terms, "sx"), "sy")
     pooled = sums / lengths.astype(jnp.float32)[:, :, None]
     return (hidden, pooled)
 

time: 493 us -> 474 us (0.961)
  waiting for transfers between devices: 326 us -> 306 us
    psum x1 -> x2, waiting for transfers between devices: 121 us -> 101 us  [shards(): sums = lax.psum(lax.psum(terms, 'sx'), 'sy')]
  transfers between devices with their start and end apart: 5 -> 6, of which waited for: 4 -> 5; matrix products, arithmetic and copies ran while one was open for 18% -> 18% of each run, Pallas kernels for 0% -> 0%
where the time goes in v1:
time: 474 us; the launch traced here: 471 us
  waiting for transfers between devices  306 us (65%)
  matrix products  73.3 us (15%)
  loops' own time  31.3 us (7%)
  local copies, waits for them, and re-layouts  25 us (5%)
  other arithmetic  15.6 us (3%)
  between operations  13.9 us (3%)
  starting transfers between devices  6 us (1%)
    all_gather x1, waiting for transfers between devices, shards(): lax.all_gather(w_qkv, 'dp', axis=0, tiled=True)  124 us
    psum x2, waiting for transfers between devices, shards(): sums = lax.psum(lax.psum(terms, 'sx'), 'sy')  101 us
    ppermute x1, waiting for transfers between devices, with_halo(): lax.ppermute(lax.slice_in_dim(block, 0, width, axis=dim), axis, backward)  51.9 us
    another operation x1, loops' own time, one_block(): outcome = lax.map(one_head, jnp.arange(heads, dtype=jnp.int32))  31.3 us
    dot_general x16, matrix products, one_head(): jnp.dot(probs, v_head, preferred_element_type=jnp.float32)  28.9 us
    ppermute x1, waiting for transfers between devices, with_halo(): lax.ppermute(lax.slice_in_dim(block, block.shape[dim] - width, None, axis...  28.8 us
    dot_general x16, matrix products, one_head(): jnp.dot(q_head, k_head.T, preferred_element_type=jnp.float32) * scale  28.1 us
    dot_general x1, matrix products, shards(): jnp.dot(normed.reshape(count_rows * local, width), qkv_full, preferred_el...  10.9 us
  transfers between devices with their start and end apart: 6, of which 5 were waited for; matrix products, arithmetic and copies ran while one was open for 18% of the time, Pallas kernels for 0%

profile of v1, /device:TPU:8, one launch (start us, length us, event | category | flops | bytes accessed | tf_op | source)
XLA Modules:
  0.0 471.2 jit_solution(6965288757414528228)
XLA Ops:
  9.2 123.8 %all-gather.3.cloned.1.call-done = bf16[1280,3840]{1,0:T(8,128)(2,1)} async-done(((bf16[640,3840]{1,0:T(8,128)(2,1)}), bf16[1280,3840]{1,0:T(8,128)(2,1)}) %all-gather.3.cloned.1.call-update) | async-done | bytes 9830416 | tf_op jit(solution)/shard_map/all_gather | solution.py:66
  133.0 10.9 %convolution_convert_fusion = bf16[512,3840]{1,0:T(8,128)(2,1)} fusion(bf16[1280,3840]{1,0:T(8,128)(2,1)} %all-gather.3.cloned.1.call-done, bf16[1,512,1280]{2,1,0:T(8,128)(2,1)S(1)} %copy-done, f32[1280]{0:T(1024)S(1)} %copy-done.4, f32[512]{0:T(512)S(1)} %add_rsqrt_fusion, f32[512]{0:T(512)S(1)} %broadcast_multiply_fusion), kind=kOutput, calls=%fused_computation.19 | convolution fusion | flops 5038407680 | bytes 15082496 | tf_op jit(solution)/shard_map/dot_general | solution.py:81
  144.0 6.3 %copy.10 = bf16[512,3840]{0,1:T(8,128)(2,1)} copy(bf16[512,3840]{1,0:T(8,128)(2,1)} %convolution_convert_fusion) | data formatting | bytes 7864320 | tf_op jit(solution)/shard_map/convert_element_type | solution.py:84
  150.3 1.9 slice.17
  152.2 2.5 collective-permute-start.1
  154.7 3.4 collective-permute-start
  158.7 2.5 slice_bitcast_fusion.2
  161.2 51.9 %collective-permute-done.1 = bf16[1,512,2,16,80]{1,4,3,2,0:T(8,128)(2,1)} collective-permute-done((bf16[1,512,2,16,80]{1,4,3,2,0:T(8,128)(2,1)S(1)}, bf16[1,512,2,16,80]{1,4,3,2,0:T(8,128)(2,1)}, u32[]{:S(2)}, u32[]{:S(2)}) %collective-permute-start.1) | collective-permute-done | bytes 2621472 | tf_op jit(solution)/shard_map/ppermute | solution.py:18
  213.0 28.8 %collective-permute-done = bf16[1,512,2,16,80]{1,4,3,2,0:T(8,128)(2,1)} collective-permute-done((bf16[1,512,2,16,80]{1,4,3,2,0:T(8,128)(2,1)S(1)}, bf16[1,512,2,16,80]{1,4,3,2,0:T(8,128)(2,1)}, u32[]{:S(2)}, u32[]{:S(2)}) %collective-permute-start) | collective-permute-done | bytes 2621472 | tf_op jit(solution)/shard_map/ppermute | solution.py:15
  241.8 3.4 pad_maximum_fusion
  245.3 3.4 slice_bitcast_fusion
  248.6 106.8 %while.18 = (s32[]{:T(128)}, bf16[16,512,80]{1,2,0:T(8,128)(2,1)S(1)}, s32[16]{0:T(128)S(1)}, bf16[512,16,80]{0,2,1:T(8,128)(2,1)}, bf16[1536,16,80]{0,2,1:T(8,1...) while((s32[]{:T(128)}, ...), condition=%wide.region_8.9_spmd.clone, body=%wide.region_5.8_spmd.clone.sunk | while | flops 258776064 | bytes 10112171 | solution.py:57
  253.5 1.8 fusion.40
  260.2 1.8 fusion.40
  266.8 1.8 fusion.40
  273.5 1.8 fusion.40
  280.2 1.8 fusion.40
  286.9 1.8 fusion.40
  293.6 1.8 fusion.40
  300.2 1.8 fusion.40
  306.9 1.8 fusion.40
  313.6 1.8 fusion.40
  320.3 1.8 fusion.40
  326.9 1.8 fusion.40
  333.6 1.8 fusion.40
  340.3 1.8 fusion.40
  347.0 1.8 fusion.40
  353.7 1.8 fusion.40
  356.5 4.2 fusion.18
  362.0 62.1 %all-reduce.3.cloned.1.call-done = f32[1,64,1280]{2,1,0:T(8,128)} async-done(((f32[1,64,1280]{2,1,0:T(8,128)}), f32[1,64,1280]{2,1,0:T(8,128)}) %all-reduce.3.cloned.1.call-update) | async-done | bytes 327696 | tf_op jit(solution)/shard_map/psum | solution.py:109
  424.2 38.7 %all-reduce.5.cloned.1.call-done = f32[1,64,1280]{2,1,0:T(8,128)} async-done(((f32[1,64,1280]{2,1,0:T(8,128)}), f32[1,64,1280]{2,1,0:T(8,128)}) %all-reduce.5.cloned.1.call-update) | async-done | bytes 327696 | tf_op jit(solution)/shard_map/psum | solution.py:109
  462.8 1.8 broadcast_divide_fusion
  (86 shorter events, 51.5 us)
Async XLA Ops:
  7.2 1.3 copy-start
  7.2 125.9 %copy-start.4 = (f32[1280]{0:T(1024)S(1)}, f32[1280]{0:T(1024)}, u32[]{:S(2)}) copy-start(f32[1280]{0:T(1024)} %param.9) | copy-start | bytes 15364
  7.2 125.9 %all-gather.3.cloned.1.call-start = ((), (), s32[]{:S(2)}) async-start(), calls=%async_computation | async-start | bytes 14745600 | tf_op jit(solution)/shard_map/all_gather | solution.py:66
  7.9 347.6 %all-gather.5.cloned.1.call-start = ((), (), s32[]{:S(2)}) async-start(), calls=%async_computation.1 | async-start | bytes 4915200 | tf_op jit(solution)/shard_map/all_gather | solution.py:67
  150.3 7.9 %copy-start.3 = (s32[1,64]{1,0:T(1,128)S(1)}, s32[1,64]{1,0:T(1,128)}, u32[]{:S(2)}) copy-start(s32[1,64]{1,0:T(1,128)} %param.8) | copy-start | bytes 772
  152.2 60.8 %collective-permute-start.1 = (bf16[1,512,2,16,80]{1,4,3,2,0:T(8,128)(2,1)S(1)}, bf16[1,512,2,16,80]{1,4,3,2,0:T(8,128)(2,1)}, u32[]{:S(2)}, u32[]{:S(2)}) collective-permute-start(bf16[1,512,2,16,80]{1,4,3,2,0:T(8,128)(2,1)S(1)} %slice.17), channel_id=1, source_target_pairs={{2,0},{4,2},{6,4},{8,6},{10,8},{12,10},{14,12},{16,14},{18,16},{20... | collective-permute-start | bytes 7864328 | tf_op jit(solution)/shard_map/ppermute | solution.py:18
  154.7 87.1 %collective-permute-start = (bf16[1,512,2,16,80]{1,4,3,2,0:T(8,128)(2,1)S(1)}, bf16[1,512,2,16,80]{1,4,3,2,0:T(8,128)(2,1)}, u32[]{:S(2)}, u32[]{:S(2)}) collective-permute-start(bf16[1,512,2,16,80]{1,4,3,2,0:T(8,128)(2,1)S(1)} %slice.17), channel_id=1, source_target_pairs={{0,2},{2,4},{4,6},{6,8},{8,10},{10,12},{12,14},{14,16},{16,18},{18... | collective-permute-start | bytes 7864328 | tf_op jit(solution)/shard_map/ppermute | solution.py:15
  158.1 266.0 %all-reduce.3.cloned.1.call-start = ((), (), s32[]{:S(2)}) async-start(), calls=%async_computation.2 | async-start | bytes 655360 | tf_op jit(solution)/shard_map/psum | solution.py:109
  245.2 3.4 copy-start.5
  248.6 107.9 %copy-start.1 = (bf16[1,512,1280]{2,1,0:T(8,128)(2,1)S(1)}, bf16[1,512,1280]{2,1,0:T(8,128)(2,1)}, u32[]{:S(2)}) copy-start(bf16[1,512,1280]{2,1,0:T(8,128)(2,1)} %param.7) | copy-start | bytes 3932164
  355.5 1.1 copy-start.6
  360.8 103.9 %copy-start.2 = (bf16[1,512,1280]{2,1,0:T(8,128)(2,1)}, bf16[1,512,1280]{2,1,0:T(8,128)(2,1)S(1)}, u32[]{:S(2)}) copy-start(bf16[1,512,1280]{2,1,0:T(8,128)(2,1)S(1)} %fusion.18) | copy-start | bytes 3932164
  361.9 100.9 %all-reduce.5.cloned.1.call-start = ((), (), s32[]{:S(2)}) async-start(), calls=%async_computation.3 | async-start | bytes 655360 | tf_op jit(solution)/shard_map/psum | solution.py:109
Sparse Core Ops, SparseCore 0:
  9.6 123.4 all-gather.2
  158.2 47.8 all-gather.4
  362.1 62.0 all-reduce.2
  426.3 36.4 all-reduce.4
